TPU v7x, 32 devices: a whole 2x2x4 slice. The times are simulated.
32 devices in a mesh: kv: 16 (over z, x, core), tp: 2 (over y).
Axes of the slice: x: 2, y: 2, z: 4, core: 2. Of those that a mesh axis runs over, the one named last changes fastest.
Arguments:
- queries: bfloat16 [16, 128, 576], P(None, 'tp'), may hold values from -36 to 36
- cache: bfloat16 [16, 4096, 576], P(None, 'kv'), may hold values from -6 to 6
- lengths: int32 [16], replicated, may hold values from 1 to 4096, as said below
- w_ov: bfloat16 [128, 512, 7168], P('tp', None, 'kv'), may hold values from -0.0234375 to 0.0234375
- resid: bfloat16 [16, 7168], P(None, 'tp'), may hold values from -3 to 3
- gain: float32 [7168], P('tp'), may hold values from 0.5 to 1.5
- w_gate: bfloat16 [7168, 18432], P('tp', 'kv'), may hold values from -0.0625 to 0.0625
- w_up: bfloat16 [7168, 18432], P('tp', 'kv'), may hold values from -0.0625 to 0.0625
- w_down: bfloat16 [18432, 7168], P('kv', 'tp'), may hold values from -0.046875 to 0.046875
Outputs:
- layer_out: bfloat16 [16, 7168], P(None, 'tp')
Inputs may be any that keep to these rules, and one draw needn't show every extreme that they name: Sequence b attends to positions 0 to lengths[b] - 1; in every draw some sequence has all 4096 positions live.
All inputs are finite; a program needn't handle non-finite values.
Results may differ from a plain program's by a relative error of at most 0.006.
Values sent between devices are 32-bit elements; how exact they have to be, the bound alone decides.
A program may use at most 128 MiB of HBM per device.

v0:
```python
import jax
import jax.numpy as jnp
from jax import lax
from jax.sharding import PartitionSpec as P

D = 7168
LAT = 512
softmax_scale = 192.0 ** (-0.5)
masked_score = -1e30
norm_floor = 0.05


def per_device(queries, cache, lengths, w_ov, resid, gain, w_gate, w_up, w_down):
    rows = cache.shape[1]
    first_row = lax.axis_index("kv") * rows
    place = first_row + lax.iota(jnp.int32, rows)
    live = (place[None, :] < lengths[:, None])[:, None, :]
    scores = (
        jnp.einsum("bhc,brc->bhr", queries, cache, preferred_element_type=jnp.float32)
        * softmax_scale
    )
    scores = jnp.where(live, scores, masked_score)
    peak = jnp.max(scores, axis=2)
    weights = jnp.where(live, jnp.exp(scores - peak[:, :, None]), 0.0)
    total = jnp.sum(weights, axis=2)
    mixed = jnp.einsum(
        "bhr,brc->bhc",
        weights.astype(jnp.bfloat16),
        cache[:, :, :LAT],
        preferred_element_type=jnp.float32,
    )
    top = lax.pmax(peak, "kv")
    factor = jnp.exp(peak - top)
    total, mixed = lax.psum((total * factor, mixed * factor[:, :, None]), "kv")
    heads_out = mixed / total[:, :, None]
    attn_part = jnp.einsum(
        "bhc,hcd->bd", heads_out.astype(jnp.bfloat16), w_ov, preferred_element_type=jnp.float32
    )
    partial_rows = lax.all_gather(attn_part, "kv", axis=1, tiled=True)
    attn = lax.psum_scatter(partial_rows, "tp", scatter_dimension=1, tiled=True)
    state = resid.astype(jnp.float32) + attn
    squares = lax.psum(jnp.sum(state * state, axis=1), "tp")
    scaled = (state * lax.rsqrt(squares / D + norm_floor)[:, None] * gain[None, :]).astype(
        jnp.bfloat16
    )
    gate_part = jnp.dot(scaled, w_gate, preferred_element_type=jnp.float32)
    up_part = jnp.dot(scaled, w_up, preferred_element_type=jnp.float32)
    gate, up = lax.psum((gate_part, up_part), "tp")
    inner = (jax.nn.silu(gate) * up).astype(jnp.bfloat16)
    ffn = lax.psum(jnp.dot(inner, w_down, preferred_element_type=jnp.float32), "kv")
    return (state + ffn).astype(jnp.bfloat16)


def solution(mesh):
    in_specs = (
        P(None, "tp", None),
        P(None, "kv", None),
        P(),
        P("tp", None, "kv"),
        P(None, "tp"),
        P("tp"),
        P("tp", "kv"),
        P("tp", "kv"),
        P("kv", "tp"),
    )
    out_specs = P(None, "tp")
    return jax.shard_map(
        per_device, mesh=mesh, in_specs=in_specs, out_specs=out_specs, check_vma=False
    )
```

profile of v0, /device:TPU:8, one launch (start us, length us, event | category | flops | bytes accessed | tf_op | source)
XLA Modules:
  0.0 339.4 jit_solution(5535327075866248540)
XLA Ops:
  6.5 0.8 broadcast_compare_fusion
  7.4 0.5 copy-done
  7.9 3.4 fusion.18
  11.3 25.9 %pmax.7 = f32[16,64]{1,0:T(8,128)S(1)} all-reduce(f32[16,64]{1,0:T(8,128)S(1)} %get-tuple-element.9), channel_id=1, replica_groups=mesh['kv'=16,'tp'=2] {'kv'}, use_global_device_ids=true, to_apply=%region_1.2 | all-reduce | flops 1024 | bytes 8192 | tf_op jit(solution)/shard_map/pmax | solution.py:32
  37.2 0.4 fusion.7
  37.6 4.9 %fusion.2 = f32[16,64,512]{2,1,0:T(8,128)} fusion(bf16[16,256,576]{1,2,0:T(8,128)(2,1)} %param.10, f32[16,64]{1,0:T(8,128)S(1)} %get-tuple-element.8, f32[16,64,256]{2,1,0:T(8,128)S(1)} %get-tuple-element.10, f32[16,64]{1,0:T(8,128)S(1)} %get-tuple-element.9, pred[16,256]{1,0:T(8,128)(4,1)S(1)} %broadcast_compare_fusion), kind=kOutput, calls=%fused_computation.3 | convolution fusion | flops 269746176 | bytes 7352320 | tf_op jit(solution)/shard_map/bhr,brc->bhc/dot_general | solution.py:26
  42.5 0.0 reduce-scatter.2.cloned.1.call-start
  42.6 30.3 %psum.43 = f32[16,64]{1,0:T(8,128)S(1)} all-reduce(f32[16,64]{1,0:T(8,128)S(1)} %get-tuple-element.7), channel_id=1, replica_groups=mesh['kv'=16,'tp'=2] {'kv'}, use_global_device_ids=true, to_apply=%region_4.5 | all-reduce | flops 1024 | bytes 8192 | tf_op jit(solution)/shard_map/psum | solution.py:34
  72.8 73.7 %all-reduce.5.cloned.1.call-done = f32[16,64,512]{2,1,0:T(8,128)} async-done(((f32[16,64,512]{2,1,0:T(8,128)}), f32[16,64,512]{2,1,0:T(8,128)}) %all-reduce.5.cloned.1.call-update) | async-done | bytes 2097168 | tf_op jit(solution)/shard_map/psum | solution.py:34
  146.5 1.8 divide_convert_fusion
  148.3 13.3 %convolution_bitcast_fusion = f32[1,448,16]{1,2,0:T(8,128)S(1)} fusion(bf16[64,512,448]{1,2,0:T(8,128)(2,1)} %param.12, bf16[16,64,512]{2,1,0:T(8,128)(2,1)S(1)} %divide_convert_fusion), kind=kOutput, calls=%fused_computation.6 | convolution fusion | flops 469762048 | bytes 30437376 | tf_op jit(solution)/shard_map/bhc,hcd->bd/dot_general | solution.py:36
  161.6 18.3 %all-gather = f32[16,448,16]{1,2,0:T(8,128)S(1)} all-gather(f32[1,448,16]{1,2,0:T(8,128)S(1)} %convolution_bitcast_fusion), channel_id=1, replica_groups=mesh['kv'=16,'tp'=2] {'kv'}, dimensions={0}, use_global_device_ids=true | all-gather | bytes 487424 | tf_op jit(solution)/shard_map/all_gather | solution.py:39
  179.9 0.3 copy.17
  180.2 1.0 reshape.33
  181.3 14.0 %reduce-scatter.2.cloned.1.call-done = f32[16,3584]{1,0:T(8,128)} async-done(((f32[16,7168]{1,0:T(8,128)}), f32[16,3584]{1,0:T(8,128)}) %reduce-scatter.2.cloned.1.call-update) | async-done | bytes 229392 | tf_op jit(solution)/shard_map/reduce_scatter | solution.py:40
  195.3 1.1 multiply_reduce_fusion
  196.3 4.9 %psum.44 = f32[16]{0:T(128)S(1)} all-reduce(f32[16]{0:T(128)S(1)} %multiply_reduce_fusion), channel_id=1, replica_groups=mesh['kv'=16,'tp'=2] {'tp'}, use_global_device_ids=true, to_apply=%region_7.8 | all-reduce | flops 16 | bytes 128 | tf_op jit(solution)/shard_map/psum | solution.py:42
  201.3 1.0 multiply_convert_fusion
  202.3 5.2 %fusion.20 = f32[16,1152]{1,0:T(8,128)} fusion(bf16[16,3584]{1,0:T(8,128)(2,1)S(1)} %multiply_convert_fusion, bf16[3584,1152]{1,0:T(8,128)(2,1)} %param.16), kind=kOutput, calls=%fused_computation.30 | convolution fusion | flops 132120576 | bytes 8445952 | tf_op jit(solution)/shard_map/dot_general | solution.py:47
  207.5 5.1 %fusion.19 = f32[16,1152]{1,0:T(8,128)} fusion(bf16[16,3584]{1,0:T(8,128)(2,1)S(1)} %multiply_convert_fusion, bf16[3584,1152]{1,0:T(8,128)(2,1)} %param.15), kind=kOutput, calls=%fused_computation.29 | convolution fusion | flops 132120576 | bytes 8445952 | tf_op jit(solution)/shard_map/dot_general | solution.py:46
  212.7 21.9 %all-reduce.9.cloned.1.call-done = (f32[16,1152]{1,0:T(8,128)}, f32[16,1152]{1,0:T(8,128)}) async-done(((f32[16,1152]{1,0:T(8,128)}, f32[16,1152]{1,0:T(8,128)}), (f32[16,1152]{1,0:T(8,128)}, f32[16,1152]{1,0:T(8,128)})) %all-reduce.9.cloned.1.call-update) | async-done | bytes 147472 | tf_op jit(solution)/shard_map/psum | solution.py:48
  234.6 5.4 %fusion.13 = f32[16,3584]{1,0:T(8,128)} fusion(bf16[1152,3584]{1,0:T(8,128)(2,1)} %param.17, f32[16,1152]{1,0:T(8,128)} %get-tuple-element.5, f32[16,1152]{1,0:T(8,128)} %get-tuple-element.6), kind=kOutput, calls=%fused_computation.19 | convolution fusion | flops 132231168 | bytes 8634368 | tf_op jit(solution)/shard_map/dot_general | solution.py:50
  240.0 91.2 %all-reduce.7.cloned.1.call-done = f32[16,3584]{1,0:T(8,128)} async-done(((f32[16,3584]{1,0:T(8,128)}), f32[16,3584]{1,0:T(8,128)}) %all-reduce.7.cloned.1.call-update) | async-done | bytes 229392 | tf_op jit(solution)/shard_map/psum | solution.py:50
  331.3 1.6 add_convert_fusion
  (19 shorter events, 0.2 us)
Async XLA Ops:
  6.5 1.3 copy-start
  6.5 140.0 %all-reduce.5.cloned.1.call-start = ((), (), s32[]{:S(2)}) async-start(), calls=%async_computation.1 | async-start | bytes 4194304 | tf_op jit(solution)/shard_map/psum | solution.py:34
  42.5 152.7 %reduce-scatter.2.cloned.1.call-start = ((), (), s32[]{:S(2)}) async-start(), calls=%async_computation.2 | async-start | bytes 688128 | tf_op jit(solution)/shard_map/reduce_scatter | solution.py:40
  148.3 46.9 %copy-start.3 = (bf16[16,3584]{1,0:T(8,128)(2,1)S(1)}, bf16[16,3584]{1,0:T(8,128)(2,1)}, u32[]{:S(2)}) copy-start(bf16[16,3584]{1,0:T(8,128)(2,1)} %param.13) | copy-start | bytes 344068
  148.3 53.0 %copy-start.4 = (f32[3584]{0:T(1024)S(1)}, f32[3584]{0:T(1024)}, u32[]{:S(2)}) copy-start(f32[3584]{0:T(1024)} %param.14) | copy-start | bytes 43012
  181.2 53.3 %all-reduce.9.cloned.1.call-start = ((), (), s32[]{:S(2)}) async-start(), calls=%async_computation.4 | async-start | bytes 294912 | tf_op jit(solution)/shard_map/psum | solution.py:48
  212.6 118.6 %all-reduce.7.cloned.1.call-start = ((), (), s32[]{:S(2)}) async-start(), calls=%async_computation.3 | async-start | bytes 458752 | tf_op jit(solution)/shard_map/psum | solution.py:50
  234.6 98.3 %copy-start.1 = (bf16[16,64,576]{2,1,0:T(8,128)(2,1)S(1)}, bf16[16,64,576]{2,1,0:T(8,128)(2,1)}, u32[]{:S(2)}) copy-start(bf16[16,64,576]{2,1,0:T(8,128)(2,1)} %param.9) | copy-start | bytes 3538948
  234.6 96.7 %copy-start.2 = (f32[16,3584]{1,0:T(8,128)S(1)}, f32[16,3584]{1,0:T(8,128)}, u32[]{:S(2)}) copy-start(f32[16,3584]{1,0:T(8,128)} %reduce-scatter.2.cloned.1.call-done) | copy-start | bytes 688132
Sparse Core Ops, SparseCore 0:
  42.6 103.8 all-reduce.4
  181.4 13.8 reduce-scatter.1
  212.8 21.7 all-reduce.8
  240.1 91.0 all-reduce.6
where the time goes:
time: 340 us; the launch traced here: 339 us
  waiting for transfers between devices  201 us (59%)
  blocking collectives  79.4 us (23%)
  matrix products  37.3 us (11%)
  between operations  13.2 us (4%)
  other arithmetic  6.8 us (2%)
    psum x1, waiting for transfers between devices, per_device(): lax.psum(jnp.dot(inner, w_down, preferred_element_type=jnp.float32), 'kv')  91.2 us
    psum x1, waiting for transfers between devices, per_device(): total, mixed = lax.psum((total * factor, mixed * factor[:, :, None]), 'kv')  73.7 us
    psum x1, blocking collectives, per_device(): total, mixed = lax.psum((total * factor, mixed * factor[:, :, None]), 'kv')  30.3 us
    pmax x1, blocking collectives, per_device(): top = lax.pmax(peak, 'kv')  25.9 us
    psum x1, waiting for transfers between devices, per_device(): gate, up = lax.psum((gate_part, up_part), 'tp')  21.9 us
    all_gather x1, blocking collectives, per_device(): partial_rows = lax.all_gather(attn_part, 'kv', axis=1, tiled=True)  18.3 us
    reduce_scatter x1, waiting for transfers between devices, per_device(): attn = lax.psum_scatter(partial_rows, 'tp', scatter_dimension=1, tiled=True)  14 us
    dot_general x1, matrix products, per_device(): jnp.einsum('bhc,hcd->bd', heads_out.astype(jnp.bfloat16), w_ov, preferred...  13.3 us
  transfers between devices with their start and end apart: 4, of which 4 were waited for; matrix products, arithmetic and copies ran while one was open for 0% of the time, Pallas kernels for 0%

commit v1 on v0

--- a/solution.py
+++ b/solution.py
@@ -47,7 +47,9 @@
     up_part = jnp.dot(scaled, w_up, preferred_element_type=jnp.float32)
     gate, up = lax.psum((gate_part, up_part), "tp")
     inner = (jax.nn.silu(gate) * up).astype(jnp.bfloat16)
-    ffn = lax.psum(jnp.dot(inner, w_down, preferred_element_type=jnp.float32), "kv")
+    ffn = jnp.sum(
+        lax.all_gather(jnp.dot(inner, w_down, preferred_element_type=jnp.float32), "kv"), axis=0
+    )
     return (state + ffn).astype(jnp.bfloat16)
 
 

time: 340 us -> 299 us (0.88)
  waiting for transfers between devices: 201 us -> 158 us
    psum x1 -> x0, waiting for transfers between devices: 91.2 us -> none  [per_device(): lax.psum(jnp.dot(inner, w_down, preferred_element_type=jnp.float32), 'kv')]
    all_gather x0 -> x1, waiting for transfers between devices: none -> 48.1 us  [per_device(): lax.all_gather(jnp.dot(inner, w_down, preferred_element_type=jnp.float32)...]
where the time goes in v1:
time: 299 us; the launch traced here: 298 us
  waiting for transfers between devices  158 us (53%)
  blocking collectives  79.4 us (27%)
  matrix products  37.3 us (12%)
  between operations  13.2 us (4%)
  other arithmetic  8.09 us (3%)
    psum x1, waiting for transfers between devices, per_device(): total, mixed = lax.psum((total * factor, mixed * factor[:, :, None]), 'kv')  73.7 us
    all_gather x1, waiting for transfers between devices, per_device(): lax.all_gather(jnp.dot(inner, w_down, preferred_element_type=jnp.float32)...  48.1 us
    psum x1, blocking collectives, per_device(): total, mixed = lax.psum((total * factor, mixed * factor[:, :, None]), 'kv')  30.3 us
    pmax x1, blocking collectives, per_device(): top = lax.pmax(peak, 'kv')  25.9 us
    psum x1, waiting for transfers between devices, per_device(): gate, up = lax.psum((gate_part, up_part), 'tp')  21.9 us
    all_gather x1, blocking collectives, per_device(): partial_rows = lax.all_gather(attn_part, 'kv', axis=1, tiled=True)  18.3 us
    reduce_scatter x1, waiting for transfers between devices, per_device(): attn = lax.psum_scatter(partial_rows, 'tp', scatter_dimension=1, tiled=True)  14 us
    dot_general x1, matrix products, per_device(): jnp.einsum('bhc,hcd->bd', heads_out.astype(jnp.bfloat16), w_ov, preferred...  13.3 us
  transfers between devices with their start and end apart: 4, of which 4 were waited for; matrix products, arithmetic and copies ran while one was open for 0% of the time, Pallas kernels for 0%

profile of v1, /device:TPU:8, one launch (start us, length us, event | category | flops | bytes accessed | tf_op | source)
XLA Modules:
  0.0 297.6 jit_solution(11099253766993231095)
XLA Ops:
  6.5 0.8 broadcast_compare_fusion
  7.4 0.5 copy-done
  7.9 3.4 %fusion.18 = (f32[16,64]{1,0:T(8,128)S(1)}, f32[16,64,256]{2,1,0:T(8,128)S(1)}) fusion(bf16[16,64,576]{2,1,0:T(8,128)(2,1)S(1)} %copy-done, bf16[16,256,576]{1,2,0:T(8,128)(2,1)} %param.10, pred[16,256]{1,0:T(8,128)(4,1)S(1)} %broadcast_compare_fusion), kind=kOutput, calls=%fused_computation.28 | convolution fusion | flops 302775296 | bytes 6955008 | tf_op jit(solution)/shard_map/bhc,brc->bhr/dot_general | solution.py:19
  11.3 25.9 %pmax.7 = f32[16,64]{1,0:T(8,128)S(1)} all-reduce(f32[16,64]{1,0:T(8,128)S(1)} %get-tuple-element.9), channel_id=1, replica_groups=mesh['kv'=16,'tp'=2] {'kv'}, use_global_device_ids=true, to_apply=%region_1.2 | all-reduce | flops 1024 | bytes 8192 | tf_op jit(solution)/shard_map/pmax | solution.py:32
  37.2 0.4 fusion.7
  37.6 4.9 %fusion.2 = f32[16,64,512]{2,1,0:T(8,128)} fusion(bf16[16,256,576]{1,2,0:T(8,128)(2,1)} %param.10, f32[16,64]{1,0:T(8,128)S(1)} %get-tuple-element.8, f32[16,64,256]{2,1,0:T(8,128)S(1)} %get-tuple-element.10, f32[16,64]{1,0:T(8,128)S(1)} %get-tuple-element.9, pred[16,256]{1,0:T(8,128)(4,1)S(1)} %broadcast_compare_fusion), kind=kOutput, calls=%fused_computation.3 | convolution fusion | flops 269746176 | bytes 7352320 | tf_op jit(solution)/shard_map/bhr,brc->bhc/dot_general | solution.py:26
  42.6 30.3 %psum.36 = f32[16,64]{1,0:T(8,128)S(1)} all-reduce(f32[16,64]{1,0:T(8,128)S(1)} %get-tuple-element.7), channel_id=1, replica_groups=mesh['kv'=16,'tp'=2] {'kv'}, use_global_device_ids=true, to_apply=%region_4.5 | all-reduce | flops 1024 | bytes 8192 | tf_op jit(solution)/shard_map/psum | solution.py:34
  72.8 73.7 %all-reduce.4.cloned.1.call-done = f32[16,64,512]{2,1,0:T(8,128)} async-done(((f32[16,64,512]{2,1,0:T(8,128)}), f32[16,64,512]{2,1,0:T(8,128)}) %all-reduce.4.cloned.1.call-update) | async-done | bytes 2097168 | tf_op jit(solution)/shard_map/psum | solution.py:34
  146.5 1.8 divide_convert_fusion
  148.3 13.3 %convolution_bitcast_fusion = f32[1,448,16]{1,2,0:T(8,128)S(1)} fusion(bf16[64,512,448]{1,2,0:T(8,128)(2,1)} %param.12, bf16[16,64,512]{2,1,0:T(8,128)(2,1)S(1)} %divide_convert_fusion), kind=kOutput, calls=%fused_computation.6 | convolution fusion | flops 469762048 | bytes 30437376 | tf_op jit(solution)/shard_map/bhc,hcd->bd/dot_general | solution.py:36
  161.6 18.3 %all-gather.1 = f32[16,448,16]{1,2,0:T(8,128)S(1)} all-gather(f32[1,448,16]{1,2,0:T(8,128)S(1)} %convolution_bitcast_fusion), channel_id=1, replica_groups=mesh['kv'=16,'tp'=2] {'kv'}, dimensions={0}, use_global_device_ids=true | all-gather | bytes 487424 | tf_op jit(solution)/shard_map/all_gather | solution.py:39
  179.9 0.3 copy.17
  180.2 1.0 reshape.34
  181.3 14.0 %reduce-scatter.2.cloned.1.call-done = f32[16,3584]{1,0:T(8,128)} async-done(((f32[16,7168]{1,0:T(8,128)}), f32[16,3584]{1,0:T(8,128)}) %reduce-scatter.2.cloned.1.call-update) | async-done | bytes 229392 | tf_op jit(solution)/shard_map/reduce_scatter | solution.py:40
  195.3 1.1 multiply_reduce_fusion
  196.3 4.9 %psum.37 = f32[16]{0:T(128)S(1)} all-reduce(f32[16]{0:T(128)S(1)} %multiply_reduce_fusion), channel_id=1, replica_groups=mesh['kv'=16,'tp'=2] {'tp'}, use_global_device_ids=true, to_apply=%region_7.8 | all-reduce | flops 16 | bytes 128 | tf_op jit(solution)/shard_map/psum | solution.py:42
  201.3 1.0 multiply_convert_fusion
  202.3 5.2 %fusion.20 = f32[16,1152]{1,0:T(8,128)} fusion(bf16[16,3584]{1,0:T(8,128)(2,1)S(1)} %multiply_convert_fusion, bf16[3584,1152]{1,0:T(8,128)(2,1)} %param.16), kind=kOutput, calls=%fused_computation.30 | convolution fusion | flops 132120576 | bytes 8445952 | tf_op jit(solution)/shard_map/dot_general | solution.py:47
  207.5 5.2 %fusion.19 = f32[16,1152]{1,0:T(8,128)} fusion(bf16[16,3584]{1,0:T(8,128)(2,1)S(1)} %multiply_convert_fusion, bf16[3584,1152]{1,0:T(8,128)(2,1)} %param.15), kind=kOutput, calls=%fused_computation.29 | convolution fusion | flops 132120576 | bytes 8445952 | tf_op jit(solution)/shard_map/dot_general | solution.py:46
  212.7 21.9 %all-reduce.6.cloned.1.call-done = (f32[16,1152]{1,0:T(8,128)}, f32[16,1152]{1,0:T(8,128)}) async-done(((f32[16,1152]{1,0:T(8,128)}, f32[16,1152]{1,0:T(8,128)}), (f32[16,1152]{1,0:T(8,128)}, f32[16,1152]{1,0:T(8,128)})) %all-reduce.6.cloned.1.call-update) | async-done | bytes 147472 | tf_op jit(solution)/shard_map/psum | solution.py:48
  234.6 5.4 %fusion.13 = f32[16,3584]{1,0:T(8,128)} fusion(bf16[1152,3584]{1,0:T(8,128)(2,1)} %param.17, f32[16,1152]{1,0:T(8,128)} %get-tuple-element.5, f32[16,1152]{1,0:T(8,128)} %get-tuple-element.6), kind=kOutput, calls=%fused_computation.19 | convolution fusion | flops 132231168 | bytes 8634368 | tf_op jit(solution)/shard_map/dot_general | solution.py:51
  240.0 48.1 %all-gather.4.cloned.1.call-done = f32[256,3584]{1,0:T(8,128)} async-done(((f32[16,3584]{1,0:T(8,128)}), f32[256,3584]{1,0:T(8,128)}) %all-gather.4.cloned.1.call-update) | async-done | bytes 3670032 | tf_op jit(solution)/shard_map/all_gather | solution.py:51
  288.1 2.2 reduce_sum.29
  290.3 0.7 add_convert_fusion
  (20 shorter events, 0.2 us)
Async XLA Ops:
  6.5 1.3 copy-start
  6.5 140.0 %all-reduce.4.cloned.1.call-start = ((), (), s32[]{:S(2)}) async-start(), calls=%async_computation.1 | async-start | bytes 4194304 | tf_op jit(solution)/shard_map/psum | solution.py:34
  42.5 152.7 %reduce-scatter.2.cloned.1.call-start = ((), (), s32[]{:S(2)}) async-start(), calls=%async_computation.2 | async-start | bytes 688128 | tf_op jit(solution)/shard_map/reduce_scatter | solution.py:40
  148.3 46.9 %copy-start.3 = (bf16[16,3584]{1,0:T(8,128)(2,1)S(1)}, bf16[16,3584]{1,0:T(8,128)(2,1)}, u32[]{:S(2)}) copy-start(bf16[16,3584]{1,0:T(8,128)(2,1)} %param.13) | copy-start | bytes 344068
  148.3 53.0 %copy-start.4 = (f32[3584]{0:T(1024)S(1)}, f32[3584]{0:T(1024)}, u32[]{:S(2)}) copy-start(f32[3584]{0:T(1024)} %param.14) | copy-start | bytes 43012
  181.2 53.4 %all-reduce.6.cloned.1.call-start = ((), (), s32[]{:S(2)}) async-start(), calls=%async_computation.4 | async-start | bytes 294912 | tf_op jit(solution)/shard_map/psum | solution.py:48
  212.7 75.4 %all-gather.4.cloned.1.call-start = ((), (), s32[]{:S(2)}) async-start(), calls=%async_computation.3 | async-start | bytes 3899392 | tf_op jit(solution)/shard_map/all_gather | solution.py:51
  234.6 55.7 %copy-start.2 = (f32[16,3584]{1,0:T(8,128)S(1)}, f32[16,3584]{1,0:T(8,128)}, u32[]{:S(2)}) copy-start(f32[16,3584]{1,0:T(8,128)} %reduce-scatter.2.cloned.1.call-done) | copy-start | bytes 688132
  234.6 56.4 %copy-start.1 = (bf16[16,64,576]{2,1,0:T(8,128)(2,1)S(1)}, bf16[16,64,576]{2,1,0:T(8,128)(2,1)}, u32[]{:S(2)}) copy-start(bf16[16,64,576]{2,1,0:T(8,128)(2,1)} %param.9) | copy-start | bytes 3538948
Sparse Core Ops, SparseCore 0:
  42.6 103.8 all-reduce.3
  181.4 13.8 reduce-scatter.1
  212.8 21.7 all-reduce.5
  240.2 47.8 all-gather.3
